TPU v7x, 32 devices: a whole 2x2x4 slice. The times are simulated.
32 devices in a mesh: member: 4 (over y, x), space: 8 (over z, core).
Axes of the slice: x: 2, y: 2, z: 4, core: 2. Of those that a mesh axis runs over, the one named last changes fastest.
Arguments:
- ensemble_prediction: bfloat16 [4, 300, 128, 128], P('member', None, 'space'), may hold values from -6 to 6
- observed_analysis: bfloat16 [300, 128, 128], P(None, 'space'), may hold values from -6 to 6
- validity_flags: int32 [2, 128, 128], P(None, 'space'), may hold values from 0 to 1, as said below
Outputs:
- point_score: float32 [300, 128, 128], P(None, 'space')
- channel_loss: float32 [300], replicated
Inputs may be any that keep to these rules, and one draw needn't show every extreme that they name: `validity_flags`: 0 or 1 for each point and group; every point of latitude row 11 is valid in both groups.
All inputs are finite; a program needn't handle non-finite values.
Results may differ from a plain program's by a relative error of at most 0.0003.
Values may be sent and summed in bfloat16 or wider, within the bound.
A program may use at most 64 MiB of HBM per device.

v0:
```python
import jax
import jax.numpy as jnp
from jax import lax
from jax.sharding import PartitionSpec as P

VARIABLE_NUMBER = 300
ATMOS = 180
TILE_SITES = 128
LON = 720
ROWS = 360


def per_channel(values):
    is_ocean = jnp.arange(VARIABLE_NUMBER, dtype=jnp.int32) >= ATMOS
    return jnp.where(is_ocean, values[1], values[0])


def shards(ensemble_prediction, observed_analysis, validity_flags):
    blocks_here = observed_analysis.shape[1]
    realization_entries = lax.axis_size("member")
    lat_rows = min(ROWS, blocks_here * lax.axis_size("space") * TILE_SITES // LON)
    first_point = lax.axis_index("space") * (blocks_here * TILE_SITES)
    position = first_point + jnp.arange(blocks_here * TILE_SITES, dtype=jnp.int32).reshape(
        blocks_here, TILE_SITES
    )
    inside = (position < lat_rows * LON).astype(jnp.float32)
    lat_row = (position // LON).astype(jnp.float32)
    cosine = jnp.cos(jnp.pi * ((lat_row + 0.5) / lat_rows - 0.5))
    valid = inside[None] * (validity_flags > 0).astype(jnp.float32)
    weight = cosine[None] * valid
    local_area = jnp.sum(weight, axis=(1, 2))
    local_count = jnp.sum(valid, axis=(1, 2))
    is_ocean = jnp.arange(VARIABLE_NUMBER, dtype=jnp.int32) >= ATMOS
    weight_chan = jnp.where(is_ocean[:, None, None], weight[1][None], weight[0][None])
    coeff = (1.0 - 0.05 / realization_entries) / (
        2.0 * realization_entries * (realization_entries - 1)
    )
    gathered = lax.all_to_all(
        ensemble_prediction, "member", split_axis=2, concat_axis=0, tiled=True
    )
    share = blocks_here // realization_entries
    first_block = lax.axis_index("member") * share
    target_part = lax.dynamic_slice_in_dim(observed_analysis, first_block, share, 1).astype(
        jnp.float32
    )
    accuracy_component = jnp.zeros(target_part.shape, jnp.float32)
    dispersion_component = jnp.zeros(target_part.shape, jnp.float32)
    for leading_realization in range(realization_entries):
        lead = gathered[leading_realization].astype(jnp.float32)
        accuracy_component = accuracy_component + jnp.abs(lead - target_part)
        for trailing_realization in range(leading_realization + 1, realization_entries):
            dispersion_component = dispersion_component + jnp.abs(
                lead - gathered[trailing_realization].astype(jnp.float32)
            )
    partial_crps = accuracy_component / realization_entries - coeff * (2.0 * dispersion_component)
    crps = lax.all_gather(partial_crps, "member", axis=1, tiled=True)
    area_sum, count = lax.psum((local_area, local_count), "space")
    scale_chan = per_channel(count / area_sum)
    point_score = crps * weight_chan * scale_chan[:, None, None]
    score_sums = lax.psum(jnp.sum(point_score, axis=(1, 2)), "space")
    channel_loss = score_sums / per_channel(count)
    return (point_score, channel_loss)


def solution(mesh):
    in_specs = (P("member", None, "space", None), P(None, "space", None), P(None, "space", None))
    out_specs = (P(None, "space", None), P())
    return jax.shard_map(shards, mesh=mesh, in_specs=in_specs, out_specs=out_specs, check_vma=False)
```

profile of v0, /device:TPU:0, one launch (start us, length us, event | category | flops | bytes accessed | tf_op | source)
XLA Modules:
  0.0 100.8 jit_solution(2808371847547564155)
XLA Ops:
  7.2 0.0 copy-start
  7.2 2.7 %copy.11 = bf16[1,300,16,128]{3,1,0,2:T(8,128)(2,1)} copy(bf16[1,300,16,128]{3,2,1,0:T(8,128)(2,1)} %param.3) | data formatting | bytes 2457600 | tf_op args[0]
  9.9 0.0 copy-start.1
  9.9 5.3 %all-to-all-start = ((bf16[1,300,16,128]{3,1,0,2:T(8,128)(2,1)}), bf16[1,300,16,128]{3,1,0,2:T(8,128)(2,1)S(1)}, u32[]{:S(2)}, u32[]{:S(2)}) async-start(bf16[1,300,16,128]{3,1,0,2:T(8,128)(2,1)} %copy.11), calls=%async_computation | async-start | bytes 2490368 | tf_op jit(solution)/shard_map/all_to_all | solution.py:38
  15.2 0.0 all-gather.2.cloned.1.call-start
  15.2 0.0 copy-done
  15.2 0.2 constant_dynamic-slice_fusion
  15.4 15.6 %all-to-all-done = bf16[1,300,16,128]{3,1,0,2:T(8,128)(2,1)S(1)} async-done(((bf16[1,300,16,128]{3,1,0,2:T(8,128)(2,1)}), bf16[1,300,16,128]{3,1,0,2:T(8,128)(2,1)S(1)}, u32[]{:S(2)}, u32[]{:S(2)}) %all-to-all-start) | async-done | bytes 1228832 | tf_op jit(solution)/shard_map/all_to_all | solution.py:38
  31.0 1.6 %fusion.5 = f32[300,4,128]{2,0,1:T(8,128)} fusion(bf16[4,1,300,4,128]{4,2,3,0,1:T(8,128)(2,1)S(1)} %bitcast.33, bf16[4,1,300,4,128]{4,2,3,1,0:T(8,128)(2,1)S(1)} %bitcast.34, bf16[300,4,128]{2,1,0:T(4,128)(2,1)S(1)} %constant_dynamic-slice_fusion), kind=kLoop, calls=%fused_computation.16 | loop fusion | flops 5529600 | bytes 2150400 | tf_op jit(solution)/shard_map/sub | solution.py:55
  32.5 0.0 all-gather.2.cloned.1.call-update
  32.6 0.1 fusion.26
  32.7 0.0 copy-done.1
  32.7 0.1 fusion.31
  32.8 0.1 select_reduce_fusion
  32.9 15.9 %all-reduce = (f32[2]{0:T(128)S(1)}, f32[2]{0:T(128)S(1)}) all-reduce(f32[2]{0:T(128)S(1)} %select_reduce_fusion, f32[2]{0:T(128)S(1)} %get-tuple-element.10), channel_id=1, replica_groups=mesh['member'=4,'space'=8] {'space'}, use_global_device_ids=true, to_apply=%region_1.2 | all-reduce | flops 4 | bytes 32 | tf_op jit(solution)/shard_map/psum | solution.py:57
  48.8 0.6 fusion.33
  49.4 1.3 %broadcast_select_fusion = f32[300]{0:T(512)S(1)} fusion(f32[]{:T(128)} %bitcast.16, f32[]{:T(128)} %bitcast.15), kind=kLoop, calls=%fused_computation.56 | loop fusion | flops 600 | bytes 1208 | tf_op jit(solution)/shard_map/jit(_where)/select_n | solution.py:15
  50.7 0.6 fusion.32
  51.3 20.2 %all-gather.2.cloned.1.call-done = f32[300,16,128]{2,0,1:T(8,128)} async-done(((f32[300,4,128]{2,0,1:T(8,128)}), f32[300,16,128]{2,0,1:T(8,128)}) %all-gather.2.cloned.1.call-update) | async-done | bytes 2457616 | tf_op jit(solution)/shard_map/all_gather | solution.py:56
  71.5 2.2 %fusion.30 = (f32[300]{0:T(512)S(1)}, f32[300,16,128]{2,0,1:T(8,128)S(1)}) fusion(f32[300]{0:T(512)S(1)} %broadcast_select_fusion, f32[300,16,128]{2,0,1:T(8,128)} %all-gather.2.cloned.1.call-done, f32[16,128]{1,0:T(8,128)S(1)} %get-tuple-element.14, f32[16,128]{1,0:T(8,128)S(1)} %get-tuple-element.13, pred[300]{0:T(512)(128)(4,1)S(1)} %iota_compare_fusion), kind=kLoop, calls=%fused_computation.58 | loop fusion | flops 2457300 | bytes 4934284 | tf_op jit(solution)/shard_map/reduce_sum | solution.py:60
  73.7 2.2 %copy.16 = f32[300,16,128]{2,1,0:T(8,128)} copy(f32[300,16,128]{2,0,1:T(8,128)S(1)} %get-tuple-element.9) | data formatting | bytes 4915200
  75.9 16.2 %psum.23 = f32[300]{0:T(512)S(1)} all-reduce(f32[300]{0:T(512)S(1)} %get-tuple-element.8), channel_id=1, replica_groups=mesh['member'=4,'space'=8] {'space'}, use_global_device_ids=true, to_apply=%region_5.6 | all-reduce | flops 300 | bytes 2400 | tf_op jit(solution)/shard_map/psum | solution.py:60
  92.1 1.9 %select_divide_fusion = f32[300]{0:T(512)} fusion(f32[300]{0:T(512)S(1)} %psum.23, f32[]{:T(128)} %bitcast.18, f32[]{:T(128)} %bitcast.17), kind=kLoop, calls=%fused_computation.54 | loop fusion | flops 900 | bytes 2408 | tf_op jit(solution)/shard_map/div | solution.py:61
  (4 shorter events, 0.0 us)
Async XLA Ops:
  7.2 8.1 %copy-start = (bf16[300,16,128]{2,1,0:T(8,128)(2,1)S(1)}, bf16[300,16,128]{2,1,0:T(8,128)(2,1)}, u32[]{:S(2)}) copy-start(bf16[300,16,128]{2,1,0:T(8,128)(2,1)} %param.4) | copy-start | bytes 3686404
  9.9 22.7 %copy-start.1 = (s32[2,16,128]{2,1,0:T(8,128)S(1)}, s32[2,16,128]{2,1,0:T(8,128)}, u32[]{:S(2)}) copy-start(s32[2,16,128]{2,1,0:T(8,128)} %param.5) | copy-start | bytes 49156
  9.9 21.1 %all-to-all-start = ((bf16[1,300,16,128]{3,1,0,2:T(8,128)(2,1)}), bf16[1,300,16,128]{3,1,0,2:T(8,128)(2,1)S(1)}, u32[]{:S(2)}, u32[]{:S(2)}) async-start(bf16[1,300,16,128]{3,1,0,2:T(8,128)(2,1)} %copy.11), calls=%async_computation | async-start | bytes 2490368 | tf_op jit(solution)/shard_map/all_to_all | solution.py:38
  15.2 56.2 %all-gather.2.cloned.1.call-start = ((), (), s32[]{:S(2)}) async-start(), calls=%async_computation.1 | async-start | bytes 3112960 | tf_op jit(solution)/shard_map/all_gather | solution.py:56
Sparse Core Ops, SparseCore 0:
  32.7 38.7 all-gather.1
where the time goes:
time: 101 us
  waiting for transfers between devices  35.8 us (35%)
  blocking collectives  32.1 us (32%)
  between operations  14.1 us (14%)
  other arithmetic  7.25 us (7%)
  local copies, waits for them, and re-layouts  6.33 us (6%)
  starting transfers between devices  5.33 us (5%)
    all_gather x1, waiting for transfers between devices, shards(): crps = lax.all_gather(partial_crps, 'member', axis=1, tiled=True)  20.2 us
    psum x1, blocking collectives, shards(): score_sums = lax.psum(jnp.sum(point_score, axis=(1, 2)), 'space')  16.2 us
    psum x1, blocking collectives, shards(): area_sum, count = lax.psum((local_area, local_count), 'space')  15.9 us
    all_to_all x1, waiting for transfers between devices, shards(): lax.all_to_all(ensemble_prediction, 'member', split_axis=2, concat_axis=0...  15.6 us
    all_to_all x1, starting transfers between devices, shards(): lax.all_to_all(ensemble_prediction, 'member', split_axis=2, concat_axis=0...  5.32 us
    unnamed x6, local copies, waits for them, and re-layouts  4.95 us
    reduce_sum x1, other arithmetic, shards(): score_sums = lax.psum(jnp.sum(point_score, axis=(1, 2)), 'space')  2.23 us
  transfers between devices with their start and end apart: 2, of which 2 were waited for; matrix products, arithmetic and copies ran while one was open for 3% of the time, Pallas kernels for 0%

commit v1 on v0

--- a/solution.py
+++ b/solution.py
@@ -8,6 +8,11 @@
 TILE_SITES = 128
 LON = 720
 ROWS = 360
+
+
+def _check_cycles(page):
+    x_now = jax.lax.all_gather(page, axis_name="space").sum(axis=0)
+    return x_now
 
 
 def per_channel(values):
@@ -57,7 +62,7 @@
     area_sum, count = lax.psum((local_area, local_count), "space")
     scale_chan = per_channel(count / area_sum)
     point_score = crps * weight_chan * scale_chan[:, None, None]
-    score_sums = lax.psum(jnp.sum(point_score, axis=(1, 2)), "space")
+    score_sums = _check_cycles(jnp.sum(point_score, axis=(1, 2)))
     channel_loss = score_sums / per_channel(count)
     return (point_score, channel_loss)
 

time: 101 us -> 114 us (1.13)
  blocking collectives: 32.1 us -> 44.3 us
  waiting for transfers between devices: 35.8 us -> 34.4 us
    unnamed x0 -> x1, blocking collectives: none -> 28.3 us
    psum x1 -> x0, blocking collectives: 16.2 us -> none  [shards(): score_sums = lax.psum(jnp.sum(point_score, axis=(1, 2)), 'space')]
    all_gather x1, waiting for transfers between devices: 20.2 us -> 18.8 us  [shards(): crps = lax.all_gather(partial_crps, 'member', axis=1, tiled=True)]
    unnamed x6 -> x11, local copies, waits for them, and re-layouts: 4.95 us -> 5.72 us
where the time goes in v1:
time: 114 us; the launch traced here: 113 us
  blocking collectives  44.3 us (39%)
  waiting for transfers between devices  34.4 us (30%)
  between operations  14.7 us (13%)
  other arithmetic  7.34 us (6%)
  local copies, waits for them, and re-layouts  7.23 us (6%)
  starting transfers between devices  5.33 us (5%)
    unnamed x1, blocking collectives  28.3 us
    all_gather x1, waiting for transfers between devices, shards(): crps = lax.all_gather(partial_crps, 'member', axis=1, tiled=True)  18.8 us
    psum x1, blocking collectives, shards(): area_sum, count = lax.psum((local_area, local_count), 'space')  15.9 us
    all_to_all x1, waiting for transfers between devices, shards(): lax.all_to_all(ensemble_prediction, 'member', split_axis=2, concat_axis=0...  15.6 us
    unnamed x11, local copies, waits for them, and re-layouts  5.72 us
    all_to_all x1, starting transfers between devices, shards(): lax.all_to_all(ensemble_prediction, 'member', split_axis=2, concat_axis=0...  5.32 us
  transfers between devices with their start and end apart: 2, of which 2 were waited for; matrix products, arithmetic and copies ran while one was open for 3% of the time, Pallas kernels for 0%

profile of v1, /device:TPU:0, one launch (start us, length us, event | category | flops | bytes accessed | tf_op | source)
XLA Modules:
  0.0 113.3 jit_solution(11325130001480963625)
XLA Ops:
  7.2 0.0 copy-start
  7.2 2.7 %copy.17 = bf16[1,300,16,128]{3,1,0,2:T(8,128)(2,1)} copy(bf16[1,300,16,128]{3,2,1,0:T(8,128)(2,1)} %param.3) | data formatting | bytes 2457600 | tf_op args[0]
  9.9 0.0 copy-start.1
  9.9 0.0 copy-start.2
  9.9 5.3 %all-to-all-start = ((bf16[1,300,16,128]{3,1,0,2:T(8,128)(2,1)}), bf16[1,300,16,128]{3,1,0,2:T(8,128)(2,1)S(1)}, u32[]{:S(2)}, u32[]{:S(2)}) async-start(bf16[1,300,16,128]{3,1,0,2:T(8,128)(2,1)} %copy.17), calls=%async_computation | async-start | bytes 2490368 | tf_op jit(solution)/shard_map/all_to_all | solution.py:43
  15.2 0.0 all-gather.3.cloned.1.call-start
  15.2 0.0 copy-done
  15.2 0.2 constant_dynamic-slice_fusion
  15.4 15.6 %all-to-all-done = bf16[1,300,16,128]{3,1,0,2:T(8,128)(2,1)S(1)} async-done(((bf16[1,300,16,128]{3,1,0,2:T(8,128)(2,1)}), bf16[1,300,16,128]{3,1,0,2:T(8,128)(2,1)S(1)}, u32[]{:S(2)}, u32[]{:S(2)}) %all-to-all-start) | async-done | bytes 1228832 | tf_op jit(solution)/shard_map/all_to_all | solution.py:43
  31.0 1.6 %fusion.5 = f32[300,4,128]{2,0,1:T(8,128)} fusion(bf16[4,1,300,4,128]{4,2,3,0,1:T(8,128)(2,1)S(1)} %bitcast.34, bf16[4,1,300,4,128]{4,2,3,1,0:T(8,128)(2,1)S(1)} %bitcast.35, bf16[300,4,128]{2,1,0:T(4,128)(2,1)S(1)} %constant_dynamic-slice_fusion), kind=kLoop, calls=%fused_computation.16 | loop fusion | flops 5529600 | bytes 2150400 | tf_op jit(solution)/shard_map/sub | solution.py:60
  32.5 0.0 all-gather.3.cloned.1.call-update
  32.6 0.1 fusion.26
  32.7 0.0 copy-done.1
  32.7 0.1 fusion.31
  32.8 0.1 select_reduce_fusion
  32.9 15.9 %all-reduce.1 = (f32[2]{0:T(128)S(1)}, f32[2]{0:T(128)S(1)}) all-reduce(f32[2]{0:T(128)S(1)} %select_reduce_fusion, f32[2]{0:T(128)S(1)} %get-tuple-element.12), channel_id=1, replica_groups=mesh['member'=4,'space'=8] {'space'}, use_global_device_ids=true, to_apply=%region_1.2 | all-reduce | flops 4 | bytes 32 | tf_op jit(solution)/shard_map/psum | solution.py:62
  48.8 0.0 copy-done.2
  48.8 0.6 dynamic-slice
  50.0 0.6 fusion.33
  50.6 1.3 %broadcast_select_fusion = f32[300]{0:T(512)S(1)} fusion(f32[]{:T(128)} %bitcast.16, f32[]{:T(128)} %bitcast.15), kind=kLoop, calls=%fused_computation.56 | loop fusion | flops 600 | bytes 1208 | tf_op jit(solution)/shard_map/jit(_where)/select_n | solution.py:20
  52.0 0.7 fusion.32
  52.7 18.8 %all-gather.3.cloned.1.call-done = f32[300,16,128]{2,0,1:T(8,128)} async-done(((f32[300,4,128]{2,0,1:T(8,128)}), f32[300,16,128]{2,0,1:T(8,128)}) %all-gather.3.cloned.1.call-update) | async-done | bytes 2457616 | tf_op jit(solution)/shard_map/all_gather | solution.py:61
  71.5 2.2 %fusion.30 = (f32[300]{0:T(512)S(1)}, f32[300,16,128]{2,0,1:T(8,128)S(1)}) fusion(f32[300]{0:T(512)S(1)} %broadcast_select_fusion, f32[300,16,128]{2,0,1:T(8,128)} %all-gather.3.cloned.1.call-done, f32[16,128]{1,0:T(8,128)S(1)} %get-tuple-element.16, f32[16,128]{1,0:T(8,128)S(1)} %get-tuple-element.15, pred[300]{0:T(512)(128)(4,1)S(1)} %iota_compare_fusion), kind=kLoop, calls=%fused_computation.58 | loop fusion | flops 2457300 | bytes 4934284 | tf_op jit(solution)/shard_map/reduce_sum | solution.py:65
  73.7 2.2 %copy.22 = f32[300,16,128]{2,1,0:T(8,128)} copy(f32[300,16,128]{2,0,1:T(8,128)S(1)} %get-tuple-element.11) | data formatting | bytes 4915200
  75.9 0.2 dynamic-update-slice
  76.1 28.3 %all-reduce = f32[2400]{0:T(1024)S(1)} all-reduce(f32[2400]{0:T(1024)S(1)} %dynamic-update-slice), channel_id=2, replica_groups=mesh['member'=4,'space'=8] {'space'}, use_global_device_ids=true, to_apply=%add | all-reduce | flops 2400 | bytes 19200
  104.4 0.1 reshape.70
  104.5 1.9 %select_divide_fusion = f32[300]{0:T(512)} fusion(f32[300]{0:T(512)S(1)} %reduce_sum.39, f32[]{:T(128)} %bitcast.19, f32[]{:T(128)} %bitcast.18), kind=kLoop, calls=%fused_computation.54 | loop fusion | flops 900 | bytes 2408 | tf_op jit(solution)/shard_map/div | solution.py:66
  (6 shorter events, 0.0 us)
Async XLA Ops:
  7.2 8.1 %copy-start = (bf16[300,16,128]{2,1,0:T(8,128)(2,1)S(1)}, bf16[300,16,128]{2,1,0:T(8,128)(2,1)}, u32[]{:S(2)}) copy-start(bf16[300,16,128]{2,1,0:T(8,128)(2,1)} %param.4) | copy-start | bytes 3686404
  9.9 22.7 %copy-start.1 = (s32[2,16,128]{2,1,0:T(8,128)S(1)}, s32[2,16,128]{2,1,0:T(8,128)}, u32[]{:S(2)}) copy-start(s32[2,16,128]{2,1,0:T(8,128)} %param.5) | copy-start | bytes 49156
  9.9 38.9 %copy-start.2 = (u32[32]{0:T(128)S(1)}, u32[32]{0:T(128)}, u32[]{:S(2)}) copy-start(u32[32]{0:T(128)} %constant.55) | copy-start | bytes 388
  9.9 21.1 %all-to-all-start = ((bf16[1,300,16,128]{3,1,0,2:T(8,128)(2,1)}), bf16[1,300,16,128]{3,1,0,2:T(8,128)(2,1)S(1)}, u32[]{:S(2)}, u32[]{:S(2)}) async-start(bf16[1,300,16,128]{3,1,0,2:T(8,128)(2,1)} %copy.17), calls=%async_computation | async-start | bytes 2490368 | tf_op jit(solution)/shard_map/all_to_all | solution.py:43
  15.2 56.2 %all-gather.3.cloned.1.call-start = ((), (), s32[]{:S(2)}) async-start(), calls=%async_computation.1 | async-start | bytes 3112960 | tf_op jit(solution)/shard_map/all_gather | solution.py:61
Sparse Core Ops, SparseCore 0:
  32.7 38.7 all-gather.2
